TPU v7x, 128 devices: a whole 4x4x4 slice. The times are simulated.
128 devices in a mesh: bank: 4 (over y_lo, core), zero: 32 (over z, y_hi, x).
Axes of the slice: x: 4, y: 4 (y_hi: 2, y_lo: 2; y = y_hi * 2 + y_lo), z: 4, core: 2. Of those that a mesh axis runs over, the one named last changes fastest.
Arguments:
- train_gate: float32 [128, 2048, 768], P('bank', 'zero'), may hold values from -0.25 to 0.25
- other_gate: bfloat16 [128, 2048, 768], P('bank', 'zero'), may hold values from -0.0625 to 0.0625
- train_up: float32 [128, 2048, 768], P('bank', 'zero'), may hold values from -0.25 to 0.25
- other_up: bfloat16 [128, 2048, 768], P('bank', 'zero'), may hold values from -0.0625 to 0.0625
- router_weight: float32 [2048, 128], P('zero', 'bank'), may hold values from -0.125 to 0.125
- router_gain: float32 [2048], P('zero'), may hold values from 0.25 to 1.75
Outputs:
- ready_gate: bfloat16 [128, 2048, 768], P(('bank', 'zero'))
- ready_up: bfloat16 [128, 2048, 768], P(('bank', 'zero'))
- scale_gate: float32 [128, 768], P(('bank', 'zero'))
- scale_up: float32 [128, 768], P(('bank', 'zero'))
- serve_router: bfloat16 [2048, 128], replicated
All inputs are finite; a program needn't handle non-finite values.
Results may differ from a plain program's by a relative error of at most 0.0075.
Values may be sent and summed in bfloat16 or wider, within the bound.
No kernel may reach another device: no remote copies, remote signals or barrier semaphores. Data moves between devices by JAX's collectives and lax.ppermute only.
A program may use at most 128 MiB of HBM per device.

v0:
```python
import jax
import jax.numpy as jnp
from jax import lax
from jax.sharding import PartitionSpec as P


def gathered_total(array, axis):
    return lax.all_gather(array, axis).astype(jnp.float32).sum(0)


def laid_out(tiles, dim):
    tiles = jnp.moveaxis(tiles, 0, dim)
    shape = tiles.shape
    return tiles.reshape(*shape[:dim], shape[dim] * shape[dim + 1], *shape[dim + 2 :])


def copy_for_each(array, axis):
    peers = lax.axis_size(axis)
    return lax.all_to_all(
        jnp.broadcast_to(array[None], (peers, *array.shape)), axis, 0, 0, tiled=True
    )


def gathered_copies(array, axis, dim):
    return laid_out(copy_for_each(array, axis), dim)


def body(train_gate, other_gate, train_up, other_up, router_weight, router_gain):
    latest_gate = train_gate + other_gate.astype(jnp.float32)
    latest_up = train_up + other_up.astype(jnp.float32)
    total_gate, total_up = (
        gathered_total(
            jnp.sum(latest_gate * latest_gate, axis=1).astype(jnp.bfloat16), "zero"
        ).astype(jnp.float32),
        gathered_total(jnp.sum(latest_up * latest_up, axis=1).astype(jnp.bfloat16), "zero").astype(
            jnp.float32
        ),
    )
    scale_gate = jnp.sqrt(total_gate)
    scale_up = jnp.sqrt(total_up)
    narrow_gate, narrow_up = (
        (latest_gate / jnp.expand_dims(scale_gate, 1)).astype(jnp.bfloat16),
        (latest_up / jnp.expand_dims(scale_up, 1)).astype(jnp.bfloat16),
    )
    ready_gate, ready_up = (
        lax.all_to_all(narrow_gate, "zero", split_axis=0, concat_axis=1, tiled=True),
        lax.all_to_all(narrow_up, "zero", split_axis=0, concat_axis=1, tiled=True),
    )
    scale_gate = lax.dynamic_slice_in_dim(
        scale_gate, lax.axis_index("zero") * ready_gate.shape[0], ready_gate.shape[0], axis=0
    )
    scale_up = lax.dynamic_slice_in_dim(
        scale_up, lax.axis_index("zero") * ready_up.shape[0], ready_up.shape[0], axis=0
    )
    part_router = (router_weight * router_gain[:, None]).astype(jnp.bfloat16)
    row_router = gathered_copies(part_router, "zero", 0)
    serve_router = gathered_copies(row_router, "bank", 1)
    return (ready_gate, ready_up, scale_gate, scale_up, serve_router)


def solution(mesh):
    placed = (
        P("bank", "zero", None),
        P("bank", "zero", None),
        P("bank", "zero", None),
        P("bank", "zero", None),
        P("zero", "bank"),
        P("zero"),
    )
    return jax.shard_map(
        body,
        mesh=mesh,
        in_specs=placed,
        out_specs=(
            P(("bank", "zero"), None, None),
            P(("bank", "zero"), None, None),
            P(("bank", "zero"), None),
            P(("bank", "zero"), None),
            P(),
        ),
        check_vma=False,
    )
```

profile of v0, /device:TPU:2, one launch (start us, length us, event | category | flops | bytes accessed | tf_op | source)
XLA Modules:
  0.0 247.7 jit_solution(13300437384595187810)
XLA Ops:
  7.2 0.0 copy-start.1
  7.2 0.0 copy-start.2
  7.2 0.0 all-gather.5.cloned.1.call-start
  7.2 5.5 %multiply_reduce_fusion.1 = bf16[32,768]{1,0:T(8,128)(2,1)} fusion(f32[32,64,768]{2,1,0:T(8,128)} %param.6, bf16[32,64,768]{2,1,0:T(8,128)(2,1)} %param.7), kind=kLoop, calls=%fused_computation.4 | loop fusion | flops 6266880 | bytes 9486336 | tf_op jit(solution)/shard_map/reduce_sum | solution.py:33
  12.7 0.0 all-gather.5.cloned.1.call-update
  12.8 0.0 copy-done.1
  12.8 0.0 copy-done.2
  12.8 0.8 reshape.49
  13.7 11.1 %all-to-all-start.2 = ((bf16[32,2,1024]{2,1,0:T(2,128)(2,1)}), bf16[32,2,1024]{2,1,0:T(2,128)(2,1)S(1)}, u32[]{:S(2)}, u32[]{:S(2)}) async-start(bf16[32,2,1024]{2,1,0:T(2,128)(2,1)} %reshape.49), calls=%async_computation.2 | async-start | bytes 262144 | tf_op jit(solution)/shard_map/all_to_all | solution.py:19
  24.8 0.0 copy-start
  24.8 0.0 all-gather.7.cloned.1.call-start
  24.8 5.7 %multiply_reduce_fusion = bf16[32,768]{1,0:T(8,128)(2,1)} fusion(f32[32,64,768]{2,1,0:T(8,128)} %param.8, bf16[32,64,768]{2,1,0:T(8,128)(2,1)} %param.9), kind=kLoop, calls=%fused_computation.1 | loop fusion | flops 6266880 | bytes 9486336 | tf_op jit(solution)/shard_map/reduce_sum | solution.py:35
  30.5 0.0 all-gather.7.cloned.1.call-update
  30.6 3.3 %all-to-all-done.2 = bf16[32,2,1024]{2,1,0:T(2,128)(2,1)S(1)} async-done(((bf16[32,2,1024]{2,1,0:T(2,128)(2,1)}), bf16[32,2,1024]{2,1,0:T(2,128)(2,1)S(1)}, u32[]{:S(2)}, u32[]{:S(2)}) %all-to-all-start.2) | async-done | bytes 131104 | tf_op jit(solution)/shard_map/all_to_all | solution.py:19
  33.8 0.2 reshape.50
  34.0 0.8 copy.16
  34.9 1.2 broadcast_in_dim.7
  36.1 0.9 broadcast_in_dim.8
  36.9 4.1 %all-to-all-start.3 = ((bf16[4,2048,32]{1,2,0:T(8,128)(2,1)}), bf16[4,2048,32]{1,2,0:T(8,128)(2,1)}, u32[]{:S(2)}, u32[]{:S(2)}) async-start(bf16[4,2048,32]{1,2,0:T(8,128)(2,1)} %broadcast_in_dim.8), calls=%async_computation.3 | async-start | bytes 1048576 | tf_op jit(solution)/shard_map/all_to_all | solution.py:19
  41.1 41.6 %all-gather.5.cloned.1.call-done = bf16[1024,768]{1,0:T(8,128)(2,1)} async-done(((bf16[32,768]{1,0:T(8,128)(2,1)}), bf16[1024,768]{1,0:T(8,128)(2,1)}) %all-gather.5.cloned.1.call-update) | async-done | bytes 1572880 | tf_op jit(solution)/shard_map/all_gather | solution.py:8
  82.7 1.6 convert_reduce_fusion.1
  84.3 0.0 copy-done
  84.4 5.6 %divide_convert_fusion.1 = bf16[32,64,768]{2,1,0:T(8,128)(2,1)} fusion(f32[32,64,768]{2,1,0:T(8,128)} %param.6, bf16[32,64,768]{2,1,0:T(8,128)(2,1)S(1)} %copy-done, f32[32,768]{1,0:T(8,128)S(1)} %sqrt.14), kind=kLoop, calls=%fused_computation.3 | loop fusion | flops 6291456 | bytes 12681216 | tf_op jit(solution)/shard_map/convert_element_type | solution.py:42
  89.9 0.0 all-to-all-done.3
  89.9 6.2 %all-to-all-start = ((bf16[32,64,768]{2,1,0:T(8,128)(2,1)}), bf16[32,64,768]{2,1,0:T(8,128)(2,1)S(1)}, u32[]{:S(2)}, u32[]{:S(2)}) async-start(bf16[32,64,768]{2,1,0:T(8,128)(2,1)} %divide_convert_fusion.1), calls=%async_computation | async-start | bytes 6291456 | tf_op jit(solution)/shard_map/all_to_all | solution.py:46
  96.1 83.6 %all-gather.7.cloned.1.call-done = bf16[1024,768]{1,0:T(8,128)(2,1)} async-done(((bf16[32,768]{1,0:T(8,128)(2,1)}), bf16[1024,768]{1,0:T(8,128)(2,1)}) %all-gather.7.cloned.1.call-update) | async-done | bytes 1572880 | tf_op jit(solution)/shard_map/all_gather | solution.py:8
  179.7 1.6 convert_reduce_fusion
  181.3 6.5 %divide_convert_fusion = bf16[32,64,768]{2,1,0:T(8,128)(2,1)} fusion(f32[32,64,768]{2,1,0:T(8,128)} %param.8, bf16[32,64,768]{2,1,0:T(8,128)(2,1)} %param.9, f32[32,768]{1,0:T(8,128)S(1)} %sqrt.15), kind=kLoop, calls=%fused_computation | loop fusion | flops 6291456 | bytes 12681216 | tf_op jit(solution)/shard_map/convert_element_type | solution.py:43
  187.8 0.0 all-to-all-done
  187.8 6.2 %all-to-all-start.1 = ((bf16[32,64,768]{2,1,0:T(8,128)(2,1)}), bf16[32,64,768]{2,1,0:T(8,128)(2,1)}, u32[]{:S(2)}, u32[]{:S(2)}) async-start(bf16[32,64,768]{2,1,0:T(8,128)(2,1)} %divide_convert_fusion), calls=%async_computation.1 | async-start | bytes 6291456 | tf_op jit(solution)/shard_map/all_to_all | solution.py:47
  194.1 2.0 copy.17
  196.1 0.6 constant_dynamic-slice_fusion
  196.7 38.8 %all-to-all-done.1 = bf16[32,64,768]{2,1,0:T(8,128)(2,1)} async-done(((bf16[32,64,768]{2,1,0:T(8,128)(2,1)}), bf16[32,64,768]{2,1,0:T(8,128)(2,1)}, u32[]{:S(2)}, u32[]{:S(2)}) %all-to-all-start.1) | async-done | bytes 3145760 | tf_op jit(solution)/shard_map/all_to_all | solution.py:47
  235.5 1.7 copy.20
  237.1 3.8 %copy.21 = bf16[1,2048,768]{2,1,0:T(8,128)(2,1)} copy(bf16[1,2048,768]{2,1,0:T(8,128)(2,1)} %bitcast.3) | data formatting | bytes 6291456
  (4 shorter events, 0.1 us)
Async XLA Ops:
  7.2 5.6 %copy-start.1 = (f32[64,32]{0,1:T(8,128)S(1)}, f32[64,32]{0,1:T(8,128)}, u32[]{:S(2)}) copy-start(f32[64,32]{0,1:T(8,128)} %param.10) | copy-start | bytes 24580
  7.2 5.6 %copy-start.2 = (f32[64]{0:T(128)S(1)}, f32[64]{0:T(128)}, u32[]{:S(2)}) copy-start(f32[64]{0:T(128)} %param.11) | copy-start | bytes 772
  7.2 75.5 %all-gather.5.cloned.1.call-start = ((), (), s32[]{:S(2)}) async-start(), calls=%async_computation.4 | async-start | bytes 1622016 | tf_op jit(solution)/shard_map/all_gather | solution.py:8
  13.7 20.1 %all-to-all-start.2 = ((bf16[32,2,1024]{2,1,0:T(2,128)(2,1)}), bf16[32,2,1024]{2,1,0:T(2,128)(2,1)S(1)}, u32[]{:S(2)}, u32[]{:S(2)}) async-start(bf16[32,2,1024]{2,1,0:T(2,128)(2,1)} %reshape.49), calls=%async_computation.2 | async-start | bytes 262144 | tf_op jit(solution)/shard_map/all_to_all | solution.py:19
  24.8 59.6 %copy-start = (bf16[32,64,768]{2,1,0:T(8,128)(2,1)S(1)}, bf16[32,64,768]{2,1,0:T(8,128)(2,1)}, u32[]{:S(2)}) copy-start(bf16[32,64,768]{2,1,0:T(8,128)(2,1)} %param.7) | copy-start | bytes 9437188
  24.8 154.9 %all-gather.7.cloned.1.call-start = ((), (), s32[]{:S(2)}) async-start(), calls=%async_computation.5 | async-start | bytes 1622016 | tf_op jit(solution)/shard_map/all_gather | solution.py:8
  36.9 53.0 %all-to-all-start.3 = ((bf16[4,2048,32]{1,2,0:T(8,128)(2,1)}), bf16[4,2048,32]{1,2,0:T(8,128)(2,1)}, u32[]{:S(2)}, u32[]{:S(2)}) async-start(bf16[4,2048,32]{1,2,0:T(8,128)(2,1)} %broadcast_in_dim.8), calls=%async_computation.3 | async-start | bytes 1048576 | tf_op jit(solution)/shard_map/all_to_all | solution.py:19
  89.9 97.9 %all-to-all-start = ((bf16[32,64,768]{2,1,0:T(8,128)(2,1)}), bf16[32,64,768]{2,1,0:T(8,128)(2,1)S(1)}, u32[]{:S(2)}, u32[]{:S(2)}) async-start(bf16[32,64,768]{2,1,0:T(8,128)(2,1)} %divide_convert_fusion.1), calls=%async_computation | async-start | bytes 6291456 | tf_op jit(solution)/shard_map/all_to_all | solution.py:46
  187.8 47.6 %all-to-all-start.1 = ((bf16[32,64,768]{2,1,0:T(8,128)(2,1)}), bf16[32,64,768]{2,1,0:T(8,128)(2,1)}, u32[]{:S(2)}, u32[]{:S(2)}) async-start(bf16[32,64,768]{2,1,0:T(8,128)(2,1)} %divide_convert_fusion), calls=%async_computation.1 | async-start | bytes 6291456 | tf_op jit(solution)/shard_map/all_to_all | solution.py:47
Sparse Core Ops, SparseCore 0:
  12.9 69.7 all-gather.4
  86.2 93.4 all-gather.6
where the time goes:
time: 248 us
  waiting for transfers between devices  167 us (67%)
  starting transfers between devices  27.7 us (11%)
  other arithmetic  26.5 us (11%)
  between operations  14.2 us (6%)
  local copies, waits for them, and re-layouts  12.1 us (5%)
    all_gather x2, waiting for transfers between devices, gathered_total(): return lax.all_gather(array, axis).astype(jnp.float32).sum(0)  125 us
    all_to_all x1, waiting for transfers between devices, body(): lax.all_to_all(narrow_up, 'zero', split_axis=0, concat_axis=1, tiled=True)  38.8 us
    all_to_all x2, starting transfers between devices, copy_for_each(): lax.all_to_all(jnp.broadcast_to(array[None], (peers, *array.shape)), axis...  15.2 us
    unnamed x12, local copies, waits for them, and re-layouts  8.58 us
    convert_element_type x1, other arithmetic, body(): (latest_up / jnp.expand_dims(scale_up, 1)).astype(jnp.bfloat16)  6.51 us
    all_to_all x1, starting transfers between devices, body(): lax.all_to_all(narrow_up, 'zero', split_axis=0, concat_axis=1, tiled=True)  6.22 us
    all_to_all x1, starting transfers between devices, body(): lax.all_to_all(narrow_gate, 'zero', split_axis=0, concat_axis=1, tiled=True)  6.17 us
    reduce_sum x1, other arithmetic, body(): jnp.sum(latest_up * latest_up, axis=1).astype(jnp.bfloat16)  5.69 us
  transfers between devices with their start and end apart: 6, of which 4 were waited for; matrix products, arithmetic and copies ran while one was open for 11% of the time, Pallas kernels for 0%

commit v1 on v0

v1 whole, which is shorter than its diff:
```python
import jax
import jax.numpy as jnp
from jax import lax
from jax.sharding import PartitionSpec as P


def regrouped(train, other):
    latest = (train + other.astype(jnp.float32)).astype(jnp.bfloat16)
    return lax.all_to_all(latest, "zero", split_axis=0, concat_axis=1, tiled=True)


def normalised(pieces):
    wide = pieces.astype(jnp.float32)
    scale = jnp.sqrt(jnp.sum(wide * wide, axis=1))
    return (wide / scale[:, None, :]).astype(jnp.bfloat16), scale


def body(train_gate, other_gate, train_up, other_up, router_weight, router_gain):
    gate = regrouped(train_gate, other_gate)
    up = regrouped(train_up, other_up)
    part_router = (router_weight * router_gain[:, None]).astype(jnp.bfloat16)
    serve_router = lax.all_gather(part_router, "zero", axis=0, tiled=True)
    serve_router = lax.all_gather(serve_router, "bank", axis=1, tiled=True)
    ready_gate, scale_gate = normalised(gate)
    ready_up, scale_up = normalised(up)
    return (ready_gate, ready_up, scale_gate, scale_up, serve_router)


def solution(mesh):
    placed = (
        P("bank", "zero", None),
        P("bank", "zero", None),
        P("bank", "zero", None),
        P("bank", "zero", None),
        P("zero", "bank"),
        P("zero"),
    )
    return jax.shard_map(
        body,
        mesh=mesh,
        in_specs=placed,
        out_specs=(
            P(("bank", "zero"), None, None),
            P(("bank", "zero"), None, None),
            P(("bank", "zero"), None),
            P(("bank", "zero"), None),
            P(),
        ),
        check_vma=False,
    )
```

time: 248 us -> 216 us (0.87)
  the two profiles are of different devices: /device:TPU:2 before, /device:TPU:1 now
where the time goes in v1:
time: 216 us; the launch traced here: 215 us
  blocking collectives  131 us (61%)
  waiting for transfers between devices  34 us (16%)
  other arithmetic  24.2 us (11%)
  starting transfers between devices  20.5 us (9%)
  local copies, waits for them, and re-layouts  5.28 us (2%)
    all_gather x1, blocking collectives, body(): serve_router = lax.all_gather(part_router, 'zero', axis=0, tiled=True)  109 us
    all_to_all x2, waiting for transfers between devices, regrouped(): lax.all_to_all(latest, 'zero', split_axis=0, concat_axis=1, tiled=True)  34 us
    all_gather x1, blocking collectives, body(): serve_router = lax.all_gather(serve_router, 'bank', axis=1, tiled=True)  21.2 us
    all_to_all x2, starting transfers between devices, regrouped(): lax.all_to_all(latest, 'zero', split_axis=0, concat_axis=1, tiled=True)  20.5 us
    convert_element_type x2, other arithmetic, regrouped(): latest = (train + other.astype(jnp.float32)).astype(jnp.bfloat16)  12.8 us
    convert_element_type x2, other arithmetic, normalised(): return ((wide / scale[:, None, :]).astype(jnp.bfloat16), scale)  4.52 us
  transfers between devices with their start and end apart: 2, of which 1 were waited for; matrix products, arithmetic and copies ran while one was open for 8% of the time, Pallas kernels for 0%

profile of v1, /device:TPU:1, one launch (start us, length us, event | category | flops | bytes accessed | tf_op | source)
XLA Modules:
  0.0 215.3 jit_solution(7930058115264093325)
XLA Ops:
  0.6 6.4 %add_convert_fusion = bf16[32,64,768]{2,1,0:T(8,128)(2,1)} fusion(f32[32,64,768]{2,1,0:T(8,128)} %param.8, bf16[32,64,768]{2,1,0:T(8,128)(2,1)} %param.9), kind=kLoop, calls=%fused_computation.5 | loop fusion | flops 4718592 | bytes 12582912 | tf_op jit(solution)/shard_map/convert_element_type | solution.py:8
  7.0 11.3 %all-to-all-start.1 = ((bf16[32,64,768]{2,1,0:T(8,128)(2,1)}), bf16[32,64,768]{2,1,0:T(8,128)(2,1)S(1)}, u32[]{:S(2)}, u32[]{:S(2)}) async-start(bf16[32,64,768]{2,1,0:T(8,128)(2,1)} %add_convert_fusion), calls=%async_computation.1 | async-start | bytes 6291456 | tf_op jit(solution)/shard_map/all_to_all | solution.py:9
  18.4 6.4 %add_convert_fusion.1 = bf16[32,64,768]{2,1,0:T(8,128)(2,1)} fusion(f32[32,64,768]{2,1,0:T(8,128)} %param.6, bf16[32,64,768]{2,1,0:T(8,128)(2,1)} %param.7), kind=kLoop, calls=%fused_computation.7 | loop fusion | flops 4718592 | bytes 12582912 | tf_op jit(solution)/shard_map/convert_element_type | solution.py:8
  24.8 0.0 copy-start.1
  24.8 0.0 copy-start.2
  24.8 34.0 %all-to-all-done.1 = bf16[32,64,768]{2,1,0:T(8,128)(2,1)S(1)} async-done(((bf16[32,64,768]{2,1,0:T(8,128)(2,1)}), bf16[32,64,768]{2,1,0:T(8,128)(2,1)S(1)}, u32[]{:S(2)}, u32[]{:S(2)}) %all-to-all-start.1) | async-done | bytes 3145760 | tf_op jit(solution)/shard_map/all_to_all | solution.py:9
  58.8 0.0 copy-start
  58.8 1.7 copy-done
  60.5 9.2 %all-to-all-start = ((bf16[32,64,768]{2,1,0:T(8,128)(2,1)}), bf16[32,64,768]{2,1,0:T(8,128)(2,1)S(1)}, u32[]{:S(2)}, u32[]{:S(2)}) async-start(bf16[32,64,768]{2,1,0:T(8,128)(2,1)} %add_convert_fusion.1), calls=%async_computation | async-start | bytes 6291456 | tf_op jit(solution)/shard_map/all_to_all | solution.py:9
  69.6 0.0 copy-done.1
  69.6 0.0 copy-done.2
  69.7 109.4 %all-gather = bf16[32,64,32]{1,2,0:T(8,128)(2,1)S(1)} all-gather(bf16[1,64,32]{1,2,0:T(8,128)(2,1)S(1)} %fusion.2), channel_id=1, replica_groups=mesh['bank'=4,'zero'=32] {'zero'}, dimensions={0}, use_global_device_ids=true | all-gather | bytes 135168 | tf_op jit(solution)/shard_map/all_gather | solution.py:22
  179.1 0.1 copy.13
  179.2 0.3 reshape.148
  179.5 21.2 %all_gather.7 = bf16[2048,128]{0,1:T(8,128)(2,1)} all-gather(bf16[2048,32]{0,1:T(8,128)(2,1)S(1)} %reshape.148), channel_id=1, replica_groups=mesh['bank'=4,'zero'=32] {'bank'}, dimensions={1}, use_global_device_ids=true | all-gather | bytes 655360 | tf_op jit(solution)/shard_map/all_gather | solution.py:23
  200.7 2.0 copy.14
  202.8 2.6 %multiply_reduce_fusion = f32[768]{0:T(1024)S(1)} fusion(bf16[32,64,768]{2,1,0:T(8,128)(2,1)} %copy-done), kind=kLoop, calls=%fused_computation.4 | loop fusion | flops 4717824 | bytes 3148800 | tf_op jit(solution)/shard_map/reduce_sum | solution.py:14
  205.4 0.6 sqrt.39
  206.0 2.7 %convert_element_type.89 = f32[32,64,768]{2,1,0:T(8,128)S(1)} convert(bf16[32,64,768]{2,1,0:T(8,128)(2,1)} %copy-done) | non-fusion elementwise | flops 1572864 | bytes 9437184 | tf_op jit(solution)/shard_map/convert_element_type | solution.py:13
  208.6 2.3 %fusion = bf16[1,2048,768]{2,1,0:T(8,128)(2,1)} fusion(f32[768]{0:T(1024)S(1)} %sqrt.37, f32[1,2048,768]{2,1,0:T(8,128)S(1)} %bitcast.14), kind=kLoop, calls=%fused_computation.1 | loop fusion | flops 3145728 | bytes 9440256 | tf_op jit(solution)/shard_map/convert_element_type | solution.py:15
  210.9 0.0 all-to-all-done
  210.9 0.7 multiply_reduce_fusion.1
  211.7 0.6 sqrt.38
  212.2 0.8 convert_element_type.88
  213.0 2.3 %fusion.1 = bf16[1,2048,768]{2,1,0:T(8,128)(2,1)} fusion(f32[768]{0:T(1024)S(1)} %sqrt.36, f32[1,2048,768]{2,1,0:T(8,128)S(1)} %bitcast.15), kind=kLoop, calls=%fused_computation.3 | loop fusion | flops 3145728 | bytes 9440256 | tf_op jit(solution)/shard_map/convert_element_type | solution.py:15
  (3 shorter events, 0.0 us)
Async XLA Ops:
  7.0 51.7 %all-to-all-start.1 = ((bf16[32,64,768]{2,1,0:T(8,128)(2,1)}), bf16[32,64,768]{2,1,0:T(8,128)(2,1)S(1)}, u32[]{:S(2)}, u32[]{:S(2)}) async-start(bf16[32,64,768]{2,1,0:T(8,128)(2,1)} %add_convert_fusion), calls=%async_computation.1 | async-start | bytes 6291456 | tf_op jit(solution)/shard_map/all_to_all | solution.py:9
  24.8 44.8 %copy-start.1 = (f32[64,32]{0,1:T(8,128)S(1)}, f32[64,32]{0,1:T(8,128)}, u32[]{:S(2)}) copy-start(f32[64,32]{0,1:T(8,128)} %param.10) | copy-start | bytes 24580
  24.8 44.8 %copy-start.2 = (f32[64]{0:T(128)S(1)}, f32[64]{0:T(128)}, u32[]{:S(2)}) copy-start(f32[64]{0:T(128)} %param.11) | copy-start | bytes 772
  58.8 1.7 copy-start
  60.5 150.5 %all-to-all-start = ((bf16[32,64,768]{2,1,0:T(8,128)(2,1)}), bf16[32,64,768]{2,1,0:T(8,128)(2,1)S(1)}, u32[]{:S(2)}, u32[]{:S(2)}) async-start(bf16[32,64,768]{2,1,0:T(8,128)(2,1)} %add_convert_fusion.1), calls=%async_computation | async-start | bytes 6291456 | tf_op jit(solution)/shard_map/all_to_all | solution.py:9

commit v2 on v1

v2 whole, which is shorter than its diff:
```python
import jax
import jax.numpy as jnp
from jax import lax
from jax.experimental import pallas as pl
from jax.experimental.pallas import tpu as pltpu
from jax.sharding import PartitionSpec as P

DESTS = 4


def latest_kernel(train_gate, other_gate, train_up, other_up, out):
    width = train_gate.shape[-1]
    out[:, :, :width] = (train_gate[...] + other_gate[...].astype(jnp.float32)).astype(jnp.bfloat16)
    out[:, :, width:] = (train_up[...] + other_up[...].astype(jnp.float32)).astype(jnp.bfloat16)


def latest_pieces(train_gate, other_gate, train_up, other_up):
    experts, rows, width = train_gate.shape
    block = pl.BlockSpec((DESTS, rows, width), lambda i: (i, 0, 0))
    return pl.pallas_call(
        latest_kernel,
        grid=(experts // DESTS,),
        in_specs=[block] * 4,
        out_specs=pl.BlockSpec((DESTS, rows, 2 * width), lambda i: (i, 0, 0)),
        out_shape=jax.ShapeDtypeStruct((experts, rows, 2 * width), jnp.bfloat16),
        name="latest_pieces",
    )(train_gate, other_gate, train_up, other_up)


LANES = 128
STEP = 256


def ready_kernel(pieces, ready, scale):
    rows = pieces.shape[0]
    for lane in range(0, pieces.shape[1], LANES):
        cols = pl.ds(lane, LANES)

        def squares(i, total):
            wide = pieces[pl.ds(i * STEP, STEP), cols].astype(jnp.float32)
            return total + jnp.sum((wide * wide).reshape(STEP // 8, 8, LANES), axis=0)

        total = lax.fori_loop(0, rows // STEP, squares, jnp.zeros((8, LANES), jnp.float32), unroll=True)
        root = jnp.sqrt(jnp.sum(total, axis=0, keepdims=True))
        scale[:, cols] = root
        inverse = 1.0 / root

        def scaled(i, carry):
            wide = pieces[pl.ds(i * STEP, STEP), cols].astype(jnp.float32)
            ready[0, pl.ds(i * STEP, STEP), cols] = (wide * inverse).astype(jnp.bfloat16)
            return carry

        lax.fori_loop(0, rows // STEP, scaled, 0, unroll=True)


BLOCK = 256


def ready_part(pieces, part):
    rows, width = pieces.shape[0], pieces.shape[1] // 2
    first = part * (width // BLOCK)
    return pl.pallas_call(
        ready_kernel,
        grid=(width // BLOCK,),
        in_specs=[pl.BlockSpec((rows, BLOCK), lambda j: (0, first + j))],
        out_specs=[
            pl.BlockSpec((1, rows, BLOCK), lambda j: (0, 0, j)),
            pl.BlockSpec((1, BLOCK), lambda j: (0, j)),
        ],
        out_shape=[
            jax.ShapeDtypeStruct((1, rows, width), jnp.bfloat16),
            jax.ShapeDtypeStruct((1, width), jnp.float32),
        ],
        name="ready_part",
    )(pieces)


def paired(array, axis, bit):
    size = lax.axis_size(axis)
    other = lax.ppermute(array, axis, [(i, i ^ bit) for i in range(size)])
    high = (lax.axis_index(axis) & bit) != 0
    return jnp.where(high, other, array), jnp.where(high, array, other)


def gathered_router(router):
    for bit in (1, 2, 4, 8, 16):
        router = jnp.concatenate(paired(router, "zero", bit), axis=1)
    router = jnp.stack(paired(router, "bank", 2))
    router = jnp.concatenate(paired(router, "bank", 1), axis=1)
    return router.reshape(-1, router.shape[-1]).T


def body(train_gate, other_gate, train_up, other_up, router_weight, router_gain):
    pieces = latest_pieces(train_gate, other_gate, train_up, other_up)
    served = lax.all_to_all(pieces, "zero", split_axis=0, concat_axis=1, tiled=True)
    served = served.reshape(served.shape[1], served.shape[2])
    router = (router_weight.T * router_gain[None, :]).astype(jnp.bfloat16)
    serve_router = gathered_router(router)
    ready_gate, scale_gate = ready_part(served, 0)
    ready_up, scale_up = ready_part(served, 1)
    return (ready_gate, ready_up, scale_gate, scale_up, serve_router)


def solution(mesh):
    placed = (
        P("bank", "zero", None),
        P("bank", "zero", None),
        P("bank", "zero", None),
        P("bank", "zero", None),
        P("zero", "bank"),
        P("zero"),
    )
    return jax.shard_map(
        body,
        mesh=mesh,
        in_specs=placed,
        out_specs=(
            P(("bank", "zero"), None, None),
            P(("bank", "zero"), None, None),
            P(("bank", "zero"), None),
            P(("bank", "zero"), None),
            P(),
        ),
        check_vma=False,
    )
```

time: 216 us -> 153 us (0.71)
  blocking collectives: 131 us -> 0 us
  waiting for transfers between devices: 34 us -> 99.3 us
  other arithmetic: 24.2 us -> 0.4 us
  Pallas kernels: 0 us -> 20.9 us
  starting transfers between devices: 20.5 us -> 29.5 us
  local copies, waits for them, and re-layouts: 5.28 us -> 1.01 us
    all_gather x2 -> x0, blocking collectives: 131 us -> none  [the longest x1 109 us: body(): serve_router = lax.all_gather(part_router, 'zero', axis=0, tiled=True)]
    ppermute x0 -> x7, waiting for transfers between devices: none -> 99.3 us  [paired(): other = lax.ppermute(array, axis, [(i, i ^ bit) for i in range(size)])]
    all_to_all x2 -> x1, waiting for transfers between devices: 34 us -> 0.01 us  [body(): lax.all_to_all(pieces, 'zero', split_axis=0, concat_axis=1, tiled=True)]
    pallas_call x0 -> x3, Pallas kernels: none -> 20.9 us  [the longest x1 10.6 us: latest_pieces(): pl.pallas_call(latest_kernel, grid=(experts // DESTS,), in_specs=[block]...]
    convert_element_type x6 -> x1, other arithmetic: 20.8 us -> 0.01 us  [body(): router = (router_weight.T * router_gain[None, :]).astype(jnp.bfloat16)]
    ppermute x0 -> x7, starting transfers between devices: none -> 17.9 us  [paired(): other = lax.ppermute(array, axis, [(i, i ^ bit) for i in range(size)])]
    all_to_all x2 -> x1, starting transfers between devices: 20.5 us -> 11.6 us  [body(): lax.all_to_all(pieces, 'zero', split_axis=0, concat_axis=1, tiled=True)]
    reduce_sum x2 -> x0, other arithmetic: 3.36 us -> none  [normalised(): scale = jnp.sqrt(jnp.sum(wide * wide, axis=1))]
  transfers between devices with their start and end apart: 2 -> 8, of which waited for: 1 -> 7; matrix products, arithmetic and copies ran while one was open for 8% -> 1% of each run, Pallas kernels for 0% -> 0%
where the time goes in v2:
time: 153 us; the launch traced here: 152 us
  waiting for transfers between devices  99.3 us (65%)
  starting transfers between devices  29.5 us (19%)
  Pallas kernels  20.9 us (14%)
    ppermute x7, waiting for transfers between devices, paired(): other = lax.ppermute(array, axis, [(i, i ^ bit) for i in range(size)])  99.3 us
    ppermute x7, starting transfers between devices, paired(): other = lax.ppermute(array, axis, [(i, i ^ bit) for i in range(size)])  17.9 us
    all_to_all x1, starting transfers between devices, body(): lax.all_to_all(pieces, 'zero', split_axis=0, concat_axis=1, tiled=True)  11.6 us
    pallas_call x1, Pallas kernels, latest_pieces(): pl.pallas_call(latest_kernel, grid=(experts // DESTS,), in_specs=[block]...  10.6 us
    pallas_call x2, Pallas kernels, ready_part(): pl.pallas_call(ready_kernel, grid=(width // BLOCK,), in_specs=[pl.BlockSp...  10.3 us
  transfers between devices with their start and end apart: 8, of which 7 were waited for; matrix products, arithmetic and copies ran while one was open for 1% of the time, Pallas kernels for 0%

profile of v2, /device:TPU:1, one launch (start us, length us, event | category | flops | bytes accessed | tf_op | source)
XLA Modules:
  0.0 151.9 jit_solution(10297257315601959160)
XLA Ops:
  0.6 10.6 %latest_pieces.1 = bf16[32,64,1536]{2,1,0:T(8,128)(2,1)} custom-call(f32[32,64,768]{2,1,0:T(8,128)} %train_gate.1, bf16[32,64,768]{2,1,0:T(8,128)(2,1)} %other_gate.1, f32[32,64,768]{2,1,0:T(8,128)} %train_up.1, bf16[32,64,768]{2,1,0:T(8,128)(2,1)} %other_up.1), custom_call_target="tpu_custom_call" | custom-call | tf_op jit(solution)/shard_map/latest_pieces/pallas_call | solution.py:20
  11.3 0.0 copy-start
  11.3 0.0 copy-start.1
  11.3 11.6 %all-to-all-start = ((bf16[32,64,1536]{2,1,0:T(8,128)(2,1)}), bf16[32,64,1536]{2,1,0:T(8,128)(2,1)}, u32[]{:S(2)}, u32[]{:S(2)}) async-start(bf16[32,64,1536]{2,1,0:T(8,128)(2,1)} %latest_pieces.1), calls=%async_computation | async-start | bytes 12582912 | tf_op jit(solution)/shard_map/all_to_all | solution.py:95
  22.9 0.0 copy-done
  22.9 0.0 copy-done.1
  22.9 1.2 collective-permute-start
  24.1 84.1 %collective-permute-done = bf16[32,64]{1,0:T(8,128)(2,1)S(1)} collective-permute-done((bf16[32,64]{1,0:T(8,128)(2,1)S(1)}, bf16[32,64]{1,0:T(8,128)(2,1)S(1)}, u32[]{:S(2)}, u32[]{:S(2)}) %collective-permute-start) | collective-permute-done | bytes 4128 | tf_op jit(solution)/shard_map/ppermute | solution.py:80
  108.2 0.1 pad_maximum_fusion.6
  108.3 2.6 %collective-permute-start.1 = (bf16[32,128]{1,0:T(8,128)(2,1)S(1)}, bf16[32,128]{1,0:T(8,128)(2,1)S(1)}, u32[]{:S(2)}, u32[]{:S(2)}) collective-permute-start(bf16[32,128]{1,0:T(8,128)(2,1)S(1)} %pad_maximum_fusion.6), channel_id=1, source_target_pairs={{0,2},{1,3},{2,0},{3,1},{4,6},{5,7},{6,4},{7,5},{8,10},{9,11},{10,... | collective-permute-start | bytes 24584 | tf_op jit(solution)/shard_map/ppermute | solution.py:80
  110.8 1.5 collective-permute-done.1
  112.3 0.1 broadcast_select_fusion.11
  112.4 6.7 %collective-permute-start.2 = (bf16[32,256]{1,0:T(8,128)(2,1)S(1)}, bf16[32,256]{1,0:T(8,128)(2,1)S(1)}, u32[]{:S(2)}, u32[]{:S(2)}) collective-permute-start(bf16[32,256]{1,0:T(8,128)(2,1)S(1)} %pad_maximum_fusion.5), channel_id=1, source_target_pairs={{0,4},{1,5},{2,6},{3,7},{4,0},{5,1},{6,2},{7,3},{8,12},{9,13},{10,... | collective-permute-start | bytes 49160 | tf_op jit(solution)/shard_map/ppermute | solution.py:80
  119.1 1.1 collective-permute-done.2
  120.3 0.1 collective-permute-start.3
  120.4 3.0 %collective-permute-done.3 = bf16[32,512]{1,0:T(8,128)(2,1)S(1)} collective-permute-done((bf16[32,512]{1,0:T(8,128)(2,1)S(1)}, bf16[32,512]{1,0:T(8,128)(2,1)S(1)}, u32[]{:S(2)}, u32[]{:S(2)}) %collective-permute-start.3) | collective-permute-done | bytes 32800 | tf_op jit(solution)/shard_map/ppermute | solution.py:80
  123.4 0.1 collective-permute-start.4
  123.5 4.6 %collective-permute-done.4 = bf16[32,1024]{1,0:T(8,128)(2,1)S(1)} collective-permute-done((bf16[32,1024]{1,0:T(8,128)(2,1)S(1)}, bf16[32,1024]{1,0:T(8,128)(2,1)S(1)}, u32[]{:S(2)}, u32[]{:S(2)}) %collective-permute-start.4) | collective-permute-done | bytes 65568 | tf_op jit(solution)/shard_map/ppermute | solution.py:80
  128.2 0.1 collective-permute-start.5
  128.3 3.8 %collective-permute-done.5 = bf16[32,2048]{1,0:T(8,128)(2,1)S(1)} collective-permute-done((bf16[32,2048]{1,0:T(8,128)(2,1)S(1)}, bf16[32,2048]{1,0:T(8,128)(2,1)S(1)}, u32[]{:S(2)}, u32[]{:S(2)}) %collective-permute-start.5) | collective-permute-done | bytes 131104 | tf_op jit(solution)/shard_map/ppermute | solution.py:80
  132.2 7.2 %collective-permute-start.6 = (bf16[2,32,2048]{2,1,0:T(8,128)(2,1)S(1)}, bf16[2,32,2048]{2,1,0:T(8,128)(2,1)S(1)}, u32[]{:S(2)}, u32[]{:S(2)}) collective-permute-start(bf16[2,32,2048]{2,1,0:T(8,128)(2,1)S(1)} %pad_maximum_fusion.1), channel_id=1, source_target_pairs={{0,32},{32,0},{64,96},{96,64},{1,33},{33,1},{65,97},{97,65},{2,34}... | collective-permute-start | bytes 786440 | tf_op jit(solution)/shard_map/ppermute | solution.py:80
  139.3 1.2 collective-permute-done.6
  140.6 1.0 copy.12
  141.6 0.0 all-to-all-done
  141.6 5.1 %ready_part.2 = (bf16[1,2048,768]{2,1,0:T(8,128)(2,1)}, f32[1,768]{1,0:T(1,128)}) custom-call(bf16[2048,1536]{1,0:T(8,128)(2,1)} %bitcast.pieces), custom_call_target="tpu_custom_call" | custom-call | tf_op jit(solution)/shard_map/ready_part/pallas_call | solution.py:62
  146.7 5.1 %ready_part.3 = (bf16[1,2048,768]{2,1,0:T(8,128)(2,1)}, f32[1,768]{1,0:T(1,128)}) custom-call(bf16[2048,1536]{1,0:T(8,128)(2,1)} %bitcast.pieces), custom_call_target="tpu_custom_call" | custom-call | tf_op jit(solution)/shard_map/ready_part/pallas_call | solution.py:62
  (13 shorter events, 0.2 us)
Async XLA Ops:
  11.3 11.6 %copy-start = (f32[64,32]{0,1:T(8,128)S(1)}, f32[64,32]{0,1:T(8,128)}, u32[]{:S(2)}) copy-start(f32[64,32]{0,1:T(8,128)} %param.10) | copy-start | bytes 24580
  11.3 11.6 %copy-start.1 = (f32[64]{0:T(128)S(1)}, f32[64]{0:T(128)}, u32[]{:S(2)}) copy-start(f32[64]{0:T(128)} %param.11) | copy-start | bytes 772
  11.3 130.3 %all-to-all-start = ((bf16[32,64,1536]{2,1,0:T(8,128)(2,1)}), bf16[32,64,1536]{2,1,0:T(8,128)(2,1)}, u32[]{:S(2)}, u32[]{:S(2)}) async-start(bf16[32,64,1536]{2,1,0:T(8,128)(2,1)} %latest_pieces.1), calls=%async_computation | async-start | bytes 12582912 | tf_op jit(solution)/shard_map/all_to_all | solution.py:95
  22.9 85.3 %collective-permute-start = (bf16[32,64]{1,0:T(8,128)(2,1)S(1)}, bf16[32,64]{1,0:T(8,128)(2,1)S(1)}, u32[]{:S(2)}, u32[]{:S(2)}) collective-permute-start(bf16[32,64]{1,0:T(8,128)(2,1)S(1)} %fusion), channel_id=1, source_target_pairs={{0,1},{1,0},{2,3},{3,2},{4,5},{5,4},{6,7},{7,6},{8,9},{9,8},{10,11... | collective-permute-start | bytes 12296 | tf_op jit(solution)/shard_map/ppermute | solution.py:80
  108.3 4.0 %collective-permute-start.1 = (bf16[32,128]{1,0:T(8,128)(2,1)S(1)}, bf16[32,128]{1,0:T(8,128)(2,1)S(1)}, u32[]{:S(2)}, u32[]{:S(2)}) collective-permute-start(bf16[32,128]{1,0:T(8,128)(2,1)S(1)} %pad_maximum_fusion.6), channel_id=1, source_target_pairs={{0,2},{1,3},{2,0},{3,1},{4,6},{5,7},{6,4},{7,5},{8,10},{9,11},{10,... | collective-permute-start | bytes 24584 | tf_op jit(solution)/shard_map/ppermute | solution.py:80
  112.4 7.8 %collective-permute-start.2 = (bf16[32,256]{1,0:T(8,128)(2,1)S(1)}, bf16[32,256]{1,0:T(8,128)(2,1)S(1)}, u32[]{:S(2)}, u32[]{:S(2)}) collective-permute-start(bf16[32,256]{1,0:T(8,128)(2,1)S(1)} %pad_maximum_fusion.5), channel_id=1, source_target_pairs={{0,4},{1,5},{2,6},{3,7},{4,0},{5,1},{6,2},{7,3},{8,12},{9,13},{10,... | collective-permute-start | bytes 49160 | tf_op jit(solution)/shard_map/ppermute | solution.py:80
  120.3 3.1 %collective-permute-start.3 = (bf16[32,512]{1,0:T(8,128)(2,1)S(1)}, bf16[32,512]{1,0:T(8,128)(2,1)S(1)}, u32[]{:S(2)}, u32[]{:S(2)}) collective-permute-start(bf16[32,512]{1,0:T(8,128)(2,1)S(1)} %pad_maximum_fusion.4), channel_id=1, source_target_pairs={{0,8},{1,9},{2,10},{3,11},{4,12},{5,13},{6,14},{7,15},{8,0},{9,1},... | collective-permute-start | bytes 98312 | tf_op jit(solution)/shard_map/ppermute | solution.py:80
  123.4 4.7 %collective-permute-start.4 = (bf16[32,1024]{1,0:T(8,128)(2,1)S(1)}, bf16[32,1024]{1,0:T(8,128)(2,1)S(1)}, u32[]{:S(2)}, u32[]{:S(2)}) collective-permute-start(bf16[32,1024]{1,0:T(8,128)(2,1)S(1)} %pad_maximum_fusion.3), channel_id=1, source_target_pairs={{0,16},{1,17},{2,18},{3,19},{4,20},{5,21},{6,22},{7,23},{8,24},{9,... | collective-permute-start | bytes 196616 | tf_op jit(solution)/shard_map/ppermute | solution.py:80
  128.2 3.9 %collective-permute-start.5 = (bf16[32,2048]{1,0:T(8,128)(2,1)S(1)}, bf16[32,2048]{1,0:T(8,128)(2,1)S(1)}, u32[]{:S(2)}, u32[]{:S(2)}) collective-permute-start(bf16[32,2048]{1,0:T(8,128)(2,1)S(1)} %pad_maximum_fusion.2), channel_id=1, source_target_pairs={{0,64},{32,96},{64,0},{96,32},{1,65},{33,97},{65,1},{97,33},{2,66}... | collective-permute-start | bytes 393224 | tf_op jit(solution)/shard_map/ppermute | solution.py:80
  132.2 8.3 %collective-permute-start.6 = (bf16[2,32,2048]{2,1,0:T(8,128)(2,1)S(1)}, bf16[2,32,2048]{2,1,0:T(8,128)(2,1)S(1)}, u32[]{:S(2)}, u32[]{:S(2)}) collective-permute-start(bf16[2,32,2048]{2,1,0:T(8,128)(2,1)S(1)} %pad_maximum_fusion.1), channel_id=1, source_target_pairs={{0,32},{32,0},{64,96},{96,64},{1,33},{33,1},{65,97},{97,65},{2,34}... | collective-permute-start | bytes 786440 | tf_op jit(solution)/shard_map/ppermute | solution.py:80

commit v3 on v1

v3 whole, which is shorter than its diff:
```python
import jax
import jax.numpy as jnp
from jax import lax
from jax.experimental import pallas as pl
from jax.experimental.pallas import tpu as pltpu
from jax.sharding import PartitionSpec as P

LANES = 128
DESTS = 2
BUFFERS = 3
MIB = 1 << 20


def latest_kernel(train_gate, other_gate, train_up, other_up, out):
    experts, rows, width = train_gate.shape
    half = rows * width // LANES
    block = pl.BlockSpec((DESTS, rows, width), lambda i: (i, 0, 0), pipeline_mode=pl.Buffered(BUFFERS))

    def step(train_gate, other_gate, train_up, other_up):
        i = pl.program_id(0)
        for start, train, other in ((0, train_gate, other_gate), (half, train_up, other_up)):
            for d in range(DESTS):
                for at in range(width // LANES):
                    cols = pl.ds(at * LANES, LANES)
                    latest = train[d, :, cols] + other[d, :, cols].astype(jnp.float32)
                    out[i * DESTS + d, start + at * rows : start + (at + 1) * rows, :] = latest.astype(jnp.bfloat16)

    pltpu.emit_pipeline(step, grid=(experts // DESTS,), in_specs=[block] * 4)(
        train_gate, other_gate, train_up, other_up
    )


def latest_pieces(arrays, total):
    experts = arrays[0].shape[0]
    return pl.pallas_call(
        latest_kernel,
        in_specs=[pl.BlockSpec(memory_space=pltpu.HBM)] * 4,
        out_specs=pl.BlockSpec(memory_space=pltpu.VMEM),
        out_shape=pltpu.VMEM((experts, total, LANES), jnp.bfloat16),
        compiler_params=pltpu.CompilerParams(vmem_limit_bytes=24 * MIB),
        name="latest_pieces",
    )(*(pltpu.with_memory_space_constraint(array, pltpu.HBM) for array in arrays))


def routed_kernel(router, pieces, out):
    out[:, out.shape[1] - router.shape[0] :, :] = jnp.broadcast_to(router[...][None], (out.shape[0], *router.shape))


def routed_pieces(router, pieces):
    return pl.pallas_call(
        routed_kernel,
        in_specs=[pl.BlockSpec(memory_space=pltpu.VMEM)] * 2,
        out_specs=pl.BlockSpec(memory_space=pltpu.VMEM),
        out_shape=pltpu.VMEM(pieces.shape, pieces.dtype),
        input_output_aliases={1: 0},
        compiler_params=pltpu.CompilerParams(vmem_limit_bytes=24 * MIB),
        name="routed_pieces",
    )(router, pieces)


def ready_block(pieces, ready, scale):
    sources, rows, _ = pieces.shape
    total = jnp.zeros((rows, LANES), jnp.float32)
    for s in range(sources):
        wide = pieces[s].astype(jnp.float32)
        total = total + wide * wide
    root = jnp.sqrt(jnp.sum(total, axis=0, keepdims=True))
    scale[...] = root
    inverse = jnp.broadcast_to(1.0 / root, (rows, LANES))
    for s in range(sources):
        wide = pieces[s].astype(jnp.float32)
        ready[0, s * rows : (s + 1) * rows, :] = (wide * inverse).astype(jnp.bfloat16)


def ready_kernel(pieces, ready_gate, ready_up, scale_gate, scale_up):
    sources = pieces.shape[0]
    rows, width = ready_gate.shape[1] // sources, ready_gate.shape[2]
    blocks = width // LANES

    def step(block, gate, up, root_gate, root_up):
        j = pl.program_id(0)

        @pl.when(j < blocks)
        def _():
            ready_block(block, gate, root_gate)

        @pl.when(j >= blocks)
        def _():
            ready_block(block, up, root_up)

    gate = lambda j: jnp.minimum(j, blocks - 1)
    up = lambda j: jnp.maximum(j - blocks, 0)
    pltpu.emit_pipeline(
        step,
        grid=(2 * blocks,),
        in_specs=[
            pl.BlockSpec((sources, rows, LANES), lambda j: (0, j, 0), pipeline_mode=pl.Buffered(BUFFERS))
        ],
        out_specs=[
            pl.BlockSpec((1, sources * rows, LANES), lambda j: (0, 0, gate(j))),
            pl.BlockSpec((1, sources * rows, LANES), lambda j: (0, 0, up(j))),
            pl.BlockSpec((1, LANES), lambda j: (0, gate(j))),
            pl.BlockSpec((1, LANES), lambda j: (0, up(j))),
        ],
    )(pieces, ready_gate, ready_up, scale_gate, scale_up)


def ready_parts(pieces, rows, width):
    ready = jax.ShapeDtypeStruct((1, pieces.shape[0] * rows, width), jnp.bfloat16)
    scale = jax.ShapeDtypeStruct((1, width), jnp.float32)
    return pl.pallas_call(
        ready_kernel,
        in_specs=[pl.BlockSpec(memory_space=pltpu.HBM)],
        out_specs=[pl.BlockSpec(memory_space=pltpu.HBM)] * 4,
        out_shape=[ready, ready, scale, scale],
        compiler_params=pltpu.CompilerParams(vmem_limit_bytes=24 * MIB),
        name="ready_parts",
    )(pieces)


def own_router_kernel(pieces, own, sem):
    cols = own.shape[1]
    copy = pltpu.make_async_copy(pieces.at[:, pl.ds(pieces.shape[1] - cols, cols)], own, sem)
    copy.start()
    copy.wait()


def own_router(pieces, cols):
    return pl.pallas_call(
        own_router_kernel,
        in_specs=[pl.BlockSpec(memory_space=pltpu.HBM)],
        out_specs=pl.BlockSpec(memory_space=pltpu.VMEM),
        out_shape=pltpu.VMEM((pieces.shape[0], cols, LANES), pieces.dtype),
        scratch_shapes=[pltpu.SemaphoreType.DMA],
        compiler_params=pltpu.CompilerParams(vmem_limit_bytes=4 * MIB),
        name="own_router",
    )(pieces)


def swapped(array, axis, bit):
    size = lax.axis_size(axis)
    return lax.ppermute(array, axis, [(i, i ^ bit) for i in range(size)])


def router_kernel(core, own, other, out):
    sources, cols, _ = own.shape
    rows = LANES // 2
    first = core[0] == 0
    for s in range(sources):
        mine, theirs = own[s].astype(jnp.float32), other[s].astype(jnp.float32)
        even, odd = jnp.where(first, mine, theirs), jnp.where(first, theirs, mine)
        tall = jnp.concatenate([even[:, :rows], odd[:, :rows], even[:, rows:], odd[:, rows:]], axis=0)
        out[s * rows : (s + 1) * rows, :] = tall.T.astype(jnp.bfloat16)


def served_router(own, other):
    sources, cols, _ = own.shape
    core = (lax.axis_index("bank") & 1).astype(jnp.int32).reshape(1)
    return pl.pallas_call(
        router_kernel,
        in_specs=[
            pl.BlockSpec(memory_space=pltpu.SMEM),
            pl.BlockSpec(memory_space=pltpu.VMEM),
            pl.BlockSpec(memory_space=pltpu.VMEM),
        ],
        out_specs=pl.BlockSpec(memory_space=pltpu.VMEM),
        out_shape=jax.ShapeDtypeStruct((sources * LANES // 2, 4 * cols), jnp.bfloat16),
        compiler_params=pltpu.CompilerParams(vmem_limit_bytes=8 * MIB),
        name="served_router",
    )(core, own, other)


def body(train_gate, other_gate, train_up, other_up, router_weight, router_gain):
    experts, rows, width = train_gate.shape
    router = (router_weight.T * router_gain[None, :]).astype(jnp.bfloat16)
    cols = router.shape[0]
    across = swapped(router, "bank", 2)
    total = 2 * rows * width // LANES + cols
    pieces = latest_pieces((train_gate, other_gate, train_up, other_up), total)
    low = (lax.axis_index("bank") & 2) == 0
    router = jnp.concatenate([jnp.where(low, router, across), jnp.where(low, across, router)], axis=1)
    pieces = routed_pieces(router, pieces)
    served = lax.all_to_all(pieces, "zero", split_axis=0, concat_axis=0, tiled=True)
    served = pltpu.with_memory_space_constraint(served, pltpu.HBM)
    own = own_router(served, cols)
    other = swapped(own, "bank", 1)
    ready_gate, ready_up, scale_gate, scale_up = ready_parts(served, rows, width)
    serve_router = served_router(own, other)
    return (ready_gate, ready_up, scale_gate, scale_up, serve_router)


def solution(mesh):
    placed = (
        P("bank", "zero", None),
        P("bank", "zero", None),
        P("bank", "zero", None),
        P("bank", "zero", None),
        P("zero", "bank"),
        P("zero"),
    )
    return jax.shard_map(
        body,
        mesh=mesh,
        in_specs=placed,
        out_specs=(
            P(("bank", "zero"), None, None),
            P(("bank", "zero"), None, None),
            P(("bank", "zero"), None),
            P(("bank", "zero"), None),
            P(),
        ),
        check_vma=False,
    )
```

time: 216 us -> 112 us (0.52)
  blocking collectives: 131 us -> 86.5 us
  waiting for transfers between devices: 34 us -> 0.01 us
  other arithmetic: 24.2 us -> 0.81 us
  Pallas kernels: 0 us -> 18.9 us
  starting transfers between devices: 20.5 us -> 4.95 us
  local copies, waits for them, and re-layouts: 5.28 us -> 0.01 us
    all_gather x2 -> x0, blocking collectives: 131 us -> none  [the longest x1 109 us: body(): serve_router = lax.all_gather(part_router, 'zero', axis=0, tiled=True)]
    all_to_all x0 -> x1, blocking collectives: none -> 86.5 us  [body(): lax.all_to_all(pieces, 'zero', split_axis=0, concat_axis=0, tiled=True)]
    all_to_all x2 -> x0, waiting for transfers between devices: 34 us -> none  [regrouped(): lax.all_to_all(latest, 'zero', split_axis=0, concat_axis=1, tiled=True)]
    all_to_all x2 -> x0, starting transfers between devices: 20.5 us -> none  [regrouped(): lax.all_to_all(latest, 'zero', split_axis=0, concat_axis=1, tiled=True)]
    convert_element_type x6 -> x1, other arithmetic: 20.8 us -> 0.73 us  [body(): router = (router_weight.T * router_gain[None, :]).astype(jnp.bfloat16)]
    pallas_call x0 -> x5, Pallas kernels: none -> 18.9 us  [the longest x1 8.56 us: latest_pieces(): pl.pallas_call(latest_kernel, in_specs=[pl.BlockSpec(memory_space=pltpu.H...]
    ppermute x0 -> x2, starting transfers between devices: none -> 4.95 us  [swapped(): return lax.ppermute(array, axis, [(i, i ^ bit) for i in range(size)])]
    unnamed x8 -> x4, local copies, waits for them, and re-layouts: 3.98 us -> 0.01 us
  transfers between devices with their start and end apart: 2 -> 2, of which waited for: 1 -> 0; matrix products, arithmetic and copies ran while one was open for 8% -> 0% of each run, Pallas kernels for 0% -> 15%
where the time goes in v3:
time: 112 us
  blocking collectives  86.5 us (77%)
  Pallas kernels  18.9 us (17%)
  starting transfers between devices  4.95 us (4%)
    all_to_all x1, blocking collectives, body(): lax.all_to_all(pieces, 'zero', split_axis=0, concat_axis=0, tiled=True)  86.5 us
    pallas_call x1, Pallas kernels, latest_pieces(): pl.pallas_call(latest_kernel, in_specs=[pl.BlockSpec(memory_space=pltpu.H...  8.56 us
    pallas_call x1, Pallas kernels, ready_parts(): pl.pallas_call(ready_kernel, in_specs=[pl.BlockSpec(memory_space=pltpu.HB...  7.79 us
    ppermute x2, starting transfers between devices, swapped(): return lax.ppermute(array, axis, [(i, i ^ bit) for i in range(size)])  4.95 us
  transfers between devices with their start and end apart: 2, of which 0 were waited for; matrix products, arithmetic and copies ran while one was open for 0% of the time, Pallas kernels for 15%

profile of v3, /device:TPU:1, one launch (start us, length us, event | category | flops | bytes accessed | tf_op | source)
XLA Modules:
  0.0 111.9 jit_solution(6372758766305500421)
XLA Ops:
  0.6 0.7 fusion
  1.4 2.1 %collective-permute-start = (bf16[32,64]{1,0:T(8,128)(2,1)S(1)}, bf16[32,64]{1,0:T(8,128)(2,1)S(1)}, u32[]{:S(2)}, u32[]{:S(2)}) collective-permute-start(bf16[32,64]{1,0:T(8,128)(2,1)S(1)} %fusion), channel_id=1, source_target_pairs={{0,64},{32,96},{64,0},{96,32},{1,65},{33,97},{65,1},{97,33},{2,66}... | collective-permute-start | bytes 12296 | tf_op jit(solution)/shard_map/ppermute | solution.py:142
  3.5 0.0 copy-start
  3.5 0.0 copy-start.1
  3.5 8.6 %latest_pieces.1.pieces = bf16[32,800,128]{2,1,0:T(8,128)(2,1)S(1)} custom-call(f32[32,64,768]{2,1,0:T(8,128)} %train_gate.1, bf16[32,64,768]{2,1,0:T(8,128)(2,1)} %other_gate.1, f32[32,64,768]{2,1,0:T(8,128)} %train_up.1, bf16[32,64,768]{2,1,0:T(8,128)(2,1)} %other_up.1), custom_call_target="tpu_custom_call" | custom-call | tf_op jit(solution)/shard_map/latest_pieces/pallas_call | solution.py:35
  12.0 0.0 collective-permute-done
  12.1 0.0 copy-done
  12.1 0.0 copy-done.1
  12.1 0.1 pad_maximum_fusion.router
  12.2 86.5 %all_to_all.5.pieces = bf16[32,800,128]{2,1,0:T(8,128)(2,1)} all-to-all(bf16[32,800,128]{2,1,0:T(8,128)(2,1)S(1)} %routed_pieces.1), channel_id=1, replica_groups=mesh['bank'=4,'zero'=32] {'zero'}, dimensions={0} | all-to-all | bytes 13107200 | tf_op jit(solution)/shard_map/all_to_all | solution.py:183
  98.7 1.0 own_router.1.own
  99.6 2.8 %collective-permute-start.1 = (bf16[32,32,128]{2,1,0:T(8,128)(2,1)S(1)}, bf16[32,32,128]{2,1,0:T(8,128)(2,1)S(1)}, u32[]{:S(2)}, u32[]{:S(2)}) collective-permute-start(bf16[32,32,128]{2,1,0:T(8,128)(2,1)S(1)} %own_router.1.own), channel_id=1, source_target_pairs={{0,32},{32,0},{64,96},{96,64},{1,33},{33,1},{65,97},{97,65},{2,34}... | collective-permute-start | bytes 786440 | tf_op jit(solution)/shard_map/ppermute | solution.py:142
  102.5 7.8 %ready_parts.1 = (bf16[1,2048,768]{2,1,0:T(8,128)(2,1)}, bf16[1,2048,768]{2,1,0:T(8,128)(2,1)}, f32[1,768]{1,0:T(1,128)}, f32[1,768]{1,0:T(1,128)}) custom-call(bf16[32,800,128]{2,1,0:T(8,128)(2,1)} %all_to_all.5.pieces), custom_call_target="tpu_custom_call" | custom-call | tf_op jit(solution)/shard_map/ready_parts/pallas_call | solution.py:111
  110.3 0.0 collective-permute-done.1.other
  110.3 1.6 %served_router.1 = bf16[2048,128]{1,0:T(8,128)(2,1)} custom-call(s32[1]{0:T(128)} %bitcast.1.core, bf16[32,32,128]{2,1,0:T(8,128)(2,1)S(1)} %own_router.1.own, bf16[32,32,128]{2,1,0:T(8,128)(2,1)S(1)} %collective-permute-done.1.other), custom_call_target="tpu_custom_call" | custom-call | tf_op jit(solution)/shard_map/served_router/pallas_call | solution.py:159
  (2 shorter events, 0.0 us)
Async XLA Ops:
  1.4 10.7 %collective-permute-start = (bf16[32,64]{1,0:T(8,128)(2,1)S(1)}, bf16[32,64]{1,0:T(8,128)(2,1)S(1)}, u32[]{:S(2)}, u32[]{:S(2)}) collective-permute-start(bf16[32,64]{1,0:T(8,128)(2,1)S(1)} %fusion), channel_id=1, source_target_pairs={{0,64},{32,96},{64,0},{96,32},{1,65},{33,97},{65,1},{97,33},{2,66}... | collective-permute-start | bytes 12296 | tf_op jit(solution)/shard_map/ppermute | solution.py:142
  3.5 8.6 %copy-start = (f32[64,32]{0,1:T(8,128)S(1)}, f32[64,32]{0,1:T(8,128)}, u32[]{:S(2)}) copy-start(f32[64,32]{0,1:T(8,128)} %param.10) | copy-start | bytes 24580
  3.5 8.6 %copy-start.1 = (f32[64]{0:T(128)S(1)}, f32[64]{0:T(128)}, u32[]{:S(2)}) copy-start(f32[64]{0:T(128)} %param.11) | copy-start | bytes 772
  99.6 10.6 %collective-permute-start.1 = (bf16[32,32,128]{2,1,0:T(8,128)(2,1)S(1)}, bf16[32,32,128]{2,1,0:T(8,128)(2,1)S(1)}, u32[]{:S(2)}, u32[]{:S(2)}) collective-permute-start(bf16[32,32,128]{2,1,0:T(8,128)(2,1)S(1)} %own_router.1.own), channel_id=1, source_target_pairs={{0,32},{32,0},{64,96},{96,64},{1,33},{33,1},{65,97},{97,65},{2,34}... | collective-permute-start | bytes 786440 | tf_op jit(solution)/shard_map/ppermute | solution.py:142

commit v4 on v1

v4 whole, which is shorter than its diff:
```python
import jax
import jax.numpy as jnp
from jax import lax
from jax.experimental import pallas as pl
from jax.experimental.pallas import tpu as pltpu
from jax.sharding import PartitionSpec as P

LANES = 128
DESTS = 4
SOURCES = 2
MIB = 1 << 20


def in_hbm(array):
    return pltpu.with_memory_space_constraint(array, pltpu.HBM)


def in_vmem(array):
    return pltpu.with_memory_space_constraint(array, pltpu.VMEM)


def latest_kernel(train_gate, other_gate, train_up, other_up, out, trains, others, sems):
    experts, rows, width = train_gate.shape
    blocks = width // LANES
    pairs = ((train_gate, trains.at[0]), (other_gate, others.at[0]), (train_up, trains.at[1]), (other_up, others.at[1]))

    def copies(i):
        at = pl.ds(i * DESTS, DESTS)
        return [pltpu.make_async_copy(hbm.at[at], vmem.at[at], sems.at[i]) for hbm, vmem in pairs]

    for i in range(experts // DESTS):
        for copy in copies(i):
            copy.start()

    def step(i, carry):
        for copy in copies(i):
            copy.wait()
        for part in range(2):
            for d in range(DESTS):
                for at in range(blocks):
                    cols = pl.ds(at * LANES, LANES)
                    e = i * DESTS + d
                    latest = trains[part, e, :, cols] + others[part, e, :, cols].astype(jnp.float32)
                    start = (part * blocks + at) * rows
                    out[e, start : start + rows, :] = latest.astype(jnp.bfloat16)
        return carry

    lax.fori_loop(0, experts // DESTS, step, 0)


def latest_pieces(arrays, total):
    experts, rows, width = arrays[0].shape
    return pl.pallas_call(
        latest_kernel,
        in_specs=[pl.BlockSpec(memory_space=pltpu.HBM)] * 4,
        out_specs=pl.BlockSpec(memory_space=pltpu.VMEM),
        out_shape=pltpu.VMEM((experts, total, LANES), jnp.bfloat16),
        scratch_shapes=[
            pltpu.VMEM((2, experts, rows, width), jnp.float32),
            pltpu.VMEM((2, experts, rows, width), jnp.bfloat16),
            pltpu.SemaphoreType.DMA((experts // DESTS,)),
        ],
        compiler_params=pltpu.CompilerParams(vmem_limit_bytes=40 * MIB),
        name="latest_pieces",
    )(*(in_hbm(array) for array in arrays))


def routed_kernel(router, pieces, out):
    out[:, out.shape[1] - router.shape[0] :, :] = jnp.broadcast_to(router[...][None], (out.shape[0], *router.shape))


def routed_pieces(router, pieces):
    return pl.pallas_call(
        routed_kernel,
        in_specs=[pl.BlockSpec(memory_space=pltpu.VMEM)] * 2,
        out_specs=pl.BlockSpec(memory_space=pltpu.VMEM),
        out_shape=pltpu.VMEM(pieces.shape, pieces.dtype),
        input_output_aliases={1: 0},
        compiler_params=pltpu.CompilerParams(vmem_limit_bytes=24 * MIB),
        name="routed_pieces",
    )(router, pieces)


def ready_kernel(pieces, ready_gate, ready_up, scale_gate, scale_up, own, buffer, sems):
    sources = pieces.shape[0]
    rows, width = ready_gate.shape[1] // sources, ready_gate.shape[2]
    blocks = width // LANES
    for part, (ready, scale) in enumerate(((ready_gate, scale_gate), (ready_up, scale_up))):
        starts = [(part * blocks + at) * rows for at in range(blocks)]
        inverses = []
        for at, start in enumerate(starts):
            total = jnp.zeros((rows, LANES), jnp.float32)
            for s in range(sources):
                wide = pieces[s, start : start + rows, :].astype(jnp.float32)
                total = total + wide * wide
            root = jnp.sqrt(jnp.sum(total, axis=0, keepdims=True))
            scale[:, at * LANES : (at + 1) * LANES] = root
            inverses.append(1.0 / root)

        def step(g, carry):
            for s in range(SOURCES):
                lines = pl.ds(pl.multiple_of((g * SOURCES + s) * rows, rows), rows)
                for at, start in enumerate(starts):
                    wide = pieces[g * SOURCES + s, start : start + rows, :].astype(jnp.float32)
                    buffer[part, lines, at * LANES : (at + 1) * LANES] = (wide * inverses[at]).astype(jnp.bfloat16)
            lines = pl.ds(pl.multiple_of(g * SOURCES * rows, SOURCES * rows), SOURCES * rows)
            pltpu.make_async_copy(buffer.at[part, lines], ready.at[0, lines], sems.at[part]).start()
            return carry

        lax.fori_loop(0, sources // SOURCES, step, 0)
    own[...] = pieces[:, 2 * blocks * rows :, :]
    for part, ready in enumerate((ready_gate, ready_up)):
        pltpu.make_async_copy(buffer.at[part], ready.at[0], sems.at[part]).wait()


def ready_parts(pieces, rows, width):
    sources, total, _ = pieces.shape
    ready = jax.ShapeDtypeStruct((1, sources * rows, width), jnp.bfloat16)
    scale = jax.ShapeDtypeStruct((1, width), jnp.float32)
    own = pltpu.VMEM((sources, total - 2 * rows * width // LANES, LANES), pieces.dtype)
    return pl.pallas_call(
        ready_kernel,
        in_specs=[pl.BlockSpec(memory_space=pltpu.VMEM)],
        out_specs=[pl.BlockSpec(memory_space=pltpu.HBM)] * 2 + [pl.BlockSpec(memory_space=pltpu.VMEM)] * 3,
        out_shape=[ready, ready, scale, scale, own],
        scratch_shapes=[
            pltpu.VMEM((2, sources * rows, width), jnp.bfloat16),
            pltpu.SemaphoreType.DMA((2,)),
        ],
        compiler_params=pltpu.CompilerParams(vmem_limit_bytes=24 * MIB),
        name="ready_parts",
    )(in_vmem(pieces))


def swapped(array, axis, bit):
    size = lax.axis_size(axis)
    return lax.ppermute(array, axis, [(i, i ^ bit) for i in range(size)])


def packed_router(weight, across, gain):
    bank = lax.axis_index("bank")
    parts = [(w * gain[:, None]).astype(jnp.bfloat16) for w in (weight, across)]
    low, even = (bank & 2) == 0, (bank & 1) == 0
    parts = [jnp.where(low, parts[0], parts[1]), jnp.where(low, parts[1], parts[0])]
    half = weight.shape[0] // 2
    groups = []
    for part in parts:
        groups += [jnp.where(even, part[:half], part[half:]), jnp.where(even, part[half:], part[:half])]
    return jnp.concatenate(groups, axis=1)


def router_kernel(odd, own, other, out):
    sources, half, _ = own.shape
    lane = lax.broadcasted_iota(jnp.int32, (half, LANES), 1)
    even_lanes = (lane // (LANES // 4)) % 2 == 0
    mine = even_lanes == (odd[0] == 0)
    for s in range(sources):
        a, b = own[s].astype(jnp.float32), other[s].astype(jnp.float32)
        first, second = jnp.where(mine, a, b), jnp.where(mine, b, a)
        left = pltpu.roll(second, LANES - LANES // 4, 1)
        right = pltpu.roll(second, LANES // 4, 1)
        out[2 * s * half : (2 * s + 1) * half, :] = first.astype(jnp.bfloat16)
        out[(2 * s + 1) * half : 2 * (s + 1) * half, :] = jnp.where(even_lanes, left, right).astype(jnp.bfloat16)


def served_router(own, other):
    sources, half, _ = own.shape
    odd = (lax.axis_index("bank") & 1).astype(jnp.int32).reshape(1)
    return pl.pallas_call(
        router_kernel,
        in_specs=[
            pl.BlockSpec(memory_space=pltpu.SMEM),
            pl.BlockSpec(memory_space=pltpu.VMEM),
            pl.BlockSpec(memory_space=pltpu.VMEM),
        ],
        out_specs=pl.BlockSpec(memory_space=pltpu.VMEM),
        out_shape=jax.ShapeDtypeStruct((2 * sources * half, LANES), jnp.bfloat16),
        compiler_params=pltpu.CompilerParams(vmem_limit_bytes=8 * MIB),
        name="served_router",
    )(odd, own, other)


def body(train_gate, other_gate, train_up, other_up, router_weight, router_gain):
    experts, rows, width = train_gate.shape
    across = swapped(router_weight.T, "bank", 2).T
    total = 2 * rows * width // LANES + rows // 2
    pieces = latest_pieces((train_gate, other_gate, train_up, other_up), total)
    pieces = routed_pieces(packed_router(router_weight, across, router_gain), pieces)
    served = lax.all_to_all(pieces, "zero", split_axis=0, concat_axis=0, tiled=True)
    ready_gate, ready_up, scale_gate, scale_up, own = ready_parts(served, rows, width)
    serve_router = served_router(own, swapped(own, "bank", 1))
    return (ready_gate, ready_up, scale_gate, scale_up, serve_router)


def solution(mesh):
    placed = (
        P("bank", "zero", None),
        P("bank", "zero", None),
        P("bank", "zero", None),
        P("bank", "zero", None),
        P("zero", "bank"),
        P("zero"),
    )
    return jax.shard_map(
        body,
        mesh=mesh,
        in_specs=placed,
        out_specs=(
            P(("bank", "zero"), None, None),
            P(("bank", "zero"), None, None),
            P(("bank", "zero"), None),
            P(("bank", "zero"), None),
            P(),
        ),
        check_vma=False,
    )
```

time: 216 us -> 105 us (0.49)
  blocking collectives: 131 us -> 86.3 us
  waiting for transfers between devices: 34 us -> 1.16 us
  other arithmetic: 24.2 us -> 0.18 us
  starting transfers between devices: 20.5 us -> 5.01 us
  Pallas kernels: 0 us -> 11.1 us
  local copies, waits for them, and re-layouts: 5.28 us -> 0.8 us
    all_gather x2 -> x0, blocking collectives: 131 us -> none  [the longest x1 109 us: body(): serve_router = lax.all_gather(part_router, 'zero', axis=0, tiled=True)]
    all_to_all x0 -> x1, blocking collectives: none -> 86.3 us  [body(): lax.all_to_all(pieces, 'zero', split_axis=0, concat_axis=0, tiled=True)]
    all_to_all x2 -> x0, waiting for transfers between devices: 34 us -> none  [regrouped(): lax.all_to_all(latest, 'zero', split_axis=0, concat_axis=1, tiled=True)]
    convert_element_type x6 -> x0, other arithmetic: 20.8 us -> none  [the longest x2 12.8 us: regrouped(): latest = (train + other.astype(jnp.float32)).astype(jnp.bfloat16)]
    all_to_all x2 -> x0, starting transfers between devices: 20.5 us -> none  [regrouped(): lax.all_to_all(latest, 'zero', split_axis=0, concat_axis=1, tiled=True)]
    pallas_call x0 -> x4, Pallas kernels: none -> 11.1 us  [the longest x1 6.62 us: latest_pieces(): pl.pallas_call(latest_kernel, in_specs=[pl.BlockSpec(memory_space=pltpu.H...]
    ppermute x0 -> x2, starting transfers between devices: none -> 5.01 us  [swapped(): return lax.ppermute(array, axis, [(i, i ^ bit) for i in range(size)])]
    reduce_sum x2 -> x0, other arithmetic: 3.36 us -> none  [normalised(): scale = jnp.sqrt(jnp.sum(wide * wide, axis=1))]
  transfers between devices with their start and end apart: 2 -> 2, of which waited for: 1 -> 1; matrix products, arithmetic and copies ran while one was open for 8% -> 0% of each run, Pallas kernels for 0% -> 6%
where the time goes in v4:
time: 105 us
  blocking collectives  86.3 us (82%)
  Pallas kernels  11.1 us (11%)
  starting transfers between devices  5.01 us (5%)
  waiting for transfers between devices  1.16 us (1%)
    all_to_all x1, blocking collectives, body(): lax.all_to_all(pieces, 'zero', split_axis=0, concat_axis=0, tiled=True)  86.3 us
    pallas_call x1, Pallas kernels, latest_pieces(): pl.pallas_call(latest_kernel, in_specs=[pl.BlockSpec(memory_space=pltpu.H...  6.62 us
    ppermute x2, starting transfers between devices, swapped(): return lax.ppermute(array, axis, [(i, i ^ bit) for i in range(size)])  5.01 us
    pallas_call x1, Pallas kernels, ready_parts(): pl.pallas_call(ready_kernel, in_specs=[pl.BlockSpec(memory_space=pltpu.VM...  3.43 us
  transfers between devices with their start and end apart: 2, of which 1 were waited for; matrix products, arithmetic and copies ran while one was open for 0% of the time, Pallas kernels for 6%

profile of v4, /device:TPU:1, one launch (start us, length us, event | category | flops | bytes accessed | tf_op | source)
XLA Modules:
  0.0 105.3 jit_solution(16309853324029426)
XLA Ops:
  0.6 0.8 copy.12
  1.4 2.2 %collective-permute-start = (f32[32,64]{0,1:T(8,128)S(1)}, f32[32,64]{0,1:T(8,128)S(1)}, u32[]{:S(2)}, u32[]{:S(2)}) collective-permute-start(f32[32,64]{0,1:T(8,128)S(1)} %bitcast.8), channel_id=1, source_target_pairs={{0,64},{32,96},{64,0},{96,32},{1,65},{33,97},{65,1},{97,33},{2,66}... | collective-permute-start | bytes 24584 | tf_op jit(solution)/shard_map/ppermute | solution.py:137
  3.6 0.0 copy-start
  3.6 6.6 %latest_pieces.1.pieces = bf16[32,800,128]{2,1,0:T(8,128)(2,1)S(1)} custom-call(f32[32,64,768]{2,1,0:T(8,128)} %train_gate.1, bf16[32,64,768]{2,1,0:T(8,128)(2,1)} %other_gate.1, f32[32,64,768]{2,1,0:T(8,128)} %train_up.1, bf16[32,64,768]{2,1,0:T(8,128)(2,1)} %other_up.1), custom_call_target="tpu_custom_call" | custom-call | tf_op jit(solution)/shard_map/latest_pieces/pallas_call | solution.py:53
  10.2 0.0 collective-permute-done
  10.2 0.0 copy-done
  10.2 0.1 broadcast_select_fusion.1
  10.4 0.1 pad_maximum_fusion.router
  10.5 86.3 %all_to_all.5.pieces = bf16[32,800,128]{2,1,0:T(8,128)(2,1)S(1)} all-to-all(bf16[32,800,128]{2,1,0:T(8,128)(2,1)S(1)} %routed_pieces.1), channel_id=1, replica_groups=mesh['bank'=4,'zero'=32] {'zero'}, dimensions={0} | all-to-all | bytes 13107200 | tf_op jit(solution)/shard_map/all_to_all | solution.py:189
  96.8 3.4 %ready_parts.1 = (bf16[1,2048,768]{2,1,0:T(8,128)(2,1)}, bf16[1,2048,768]{2,1,0:T(8,128)(2,1)}, f32[1,768]{1,0:T(1,128)}, f32[1,768]{1,0:T(1,128)}, bf16[32,32,128]{2,1,0:T(8,128)(2,1)S(1)}) custom-call(bf16[32,800,128]{2,1,0:T(8,128)(2,1)S(1)} %all_to_all.5.pieces), custom_call_target="tpu_custom_call" | custom-call | tf_op jit(solution)/shard_map/ready_parts/pallas_call | solution.py:121
  100.3 2.8 %collective-permute-start.1 = (bf16[32,32,128]{2,1,0:T(8,128)(2,1)S(1)}, bf16[32,32,128]{2,1,0:T(8,128)(2,1)S(1)}, u32[]{:S(2)}, u32[]{:S(2)}) collective-permute-start(bf16[32,32,128]{2,1,0:T(8,128)(2,1)S(1)} %get-tuple-element.14.own), channel_id=1, source_target_pairs={{0,32},{32,0},{64,96},{96,64},{1,33},{33,1},{65,97},{97,65},{2,34}... | collective-permute-start | bytes 786440 | tf_op jit(solution)/shard_map/ppermute | solution.py:137
  103.1 1.2 %collective-permute-done.1.other = bf16[32,32,128]{2,1,0:T(8,128)(2,1)S(1)} collective-permute-done((bf16[32,32,128]{2,1,0:T(8,128)(2,1)S(1)}, bf16[32,32,128]{2,1,0:T(8,128)(2,1)S(1)}, u32[]{:S(2)}, u32[]{:S(2)}) %collective-permute-start.1) | collective-permute-done | bytes 262176 | tf_op jit(solution)/shard_map/ppermute | solution.py:137
  104.3 1.0 served_router.1
  (2 shorter events, 0.0 us)
Async XLA Ops:
  1.4 8.8 %collective-permute-start = (f32[32,64]{0,1:T(8,128)S(1)}, f32[32,64]{0,1:T(8,128)S(1)}, u32[]{:S(2)}, u32[]{:S(2)}) collective-permute-start(f32[32,64]{0,1:T(8,128)S(1)} %bitcast.8), channel_id=1, source_target_pairs={{0,64},{32,96},{64,0},{96,32},{1,65},{33,97},{65,1},{97,33},{2,66}... | collective-permute-start | bytes 24584 | tf_op jit(solution)/shard_map/ppermute | solution.py:137
  3.6 6.6 %copy-start = (f32[64]{0:T(128)S(1)}, f32[64]{0:T(128)}, u32[]{:S(2)}) copy-start(f32[64]{0:T(128)} %param.11) | copy-start | bytes 772
  100.3 4.0 %collective-permute-start.1 = (bf16[32,32,128]{2,1,0:T(8,128)(2,1)S(1)}, bf16[32,32,128]{2,1,0:T(8,128)(2,1)S(1)}, u32[]{:S(2)}, u32[]{:S(2)}) collective-permute-start(bf16[32,32,128]{2,1,0:T(8,128)(2,1)S(1)} %get-tuple-element.14.own), channel_id=1, source_target_pairs={{0,32},{32,0},{64,96},{96,64},{1,33},{33,1},{65,97},{97,65},{2,34}... | collective-permute-start | bytes 786440 | tf_op jit(solution)/shard_map/ppermute | solution.py:137
